TPU v7x, 32 devices: a whole 2x2x4 slice. The times are simulated.
32 devices in a mesh: group: 4 (over z), tensor: 8 (over y, x, core).
Axes of the slice: x: 2, y: 2, z: 4, core: 2. Of those that a mesh axis runs over, the one named last changes fastest.
Arguments:
- key_value_cache: bfloat16 [256, 1024, 256], P(('group', 'tensor')), may hold values from -8 to 8
- queries: bfloat16 [32, 48, 128], P('group'), may hold values from -200 to 200
- fresh_key_value: bfloat16 [32, 8, 256], P('group'), may hold values from -6 to 6
- lengths: int32 [32], P('group'), may hold values from 2 to 1023
- residual: bfloat16 [32, 6144], P('group'), may hold values from -100 to 100
- norm_gain: float32 [6144], replicated, may hold values from 0.1 to 1.9
- router_weight: bfloat16 [6144, 8], replicated, may hold values from -0.078125 to 0.078125
- routing: int32 [32, 2], P('group'), may hold values from 0 to 7, all different within a row
- expert_gate: bfloat16 [8, 6144, 8192], P(None, 'group', 'tensor'), may hold values from -0.078125 to 0.078125
- expert_up: bfloat16 [8, 6144, 8192], P(None, 'group', 'tensor'), may hold values from -0.078125 to 0.078125
Outputs:
- updated: bfloat16 [32, 6144], P('group')
- expert_hidden: bfloat16 [32, 2, 8192], P('group', None, 'tensor')
- new_cache: bfloat16 [32, 8, 1024, 256], P('group', None, 'tensor')
Inputs may be any that keep to these rules, and one draw needn't show every extreme that they name: Slot lengths[s] of sequence s receives its new token. `routing`: A token's two experts differ.
All inputs are finite; a program needn't handle non-finite values.
Results may differ from a plain program's by a relative error of at most 0.028.
Values may be sent and summed in bfloat16 or wider, within the bound.
No kernel may reach another device: no remote copies, remote signals or barrier semaphores. Data moves between devices by JAX's collectives and lax.ppermute only.
A program may use at most 128 MiB of HBM per device.

v0:
```python
import math
import jax
import jax.numpy as jnp
from jax import lax
from jax.sharding import PartitionSpec as P


def body(
    key_value_cache,
    queries,
    fresh_key_value,
    lengths,
    residual,
    norm_gain,
    router_weight,
    routing,
    expert_gate,
    expert_up,
):
    tensor_rank = lax.axis_index("tensor")
    seq_local = queries.shape[0]
    q_heads = queries.shape[1]
    kv_heads = fresh_key_value.shape[1]
    head_size = fresh_key_value.shape[2] // 2
    query_group_width = q_heads // kv_heads
    score_scale = 1.0 / math.sqrt(head_size)
    arrived = lax.all_to_all(key_value_cache, "tensor", split_axis=1, concat_axis=0, tiled=True)
    local_span = arrived.shape[1]
    arrived = arrived.reshape(seq_local, kv_heads, local_span, 2 * head_size)
    slot_index = tensor_rank * local_span + lax.broadcasted_iota(jnp.int32, (local_span,), 0)
    new_slot = slot_index[None, None, :, None] == lengths[:, None, None, None]
    new_cache = jnp.where(new_slot, fresh_key_value[:, :, None, :], arrived)
    pair_count = key_value_cache.shape[0]
    pair_begin = tensor_rank * pair_count
    query_vectors = lax.dynamic_slice_in_dim(
        queries.reshape(seq_local * kv_heads, query_group_width, head_size),
        pair_begin,
        pair_count,
        0,
    )
    own_rows = lax.dynamic_slice_in_dim(
        fresh_key_value.reshape(seq_local * kv_heads, 2 * head_size), pair_begin, pair_count, 0
    )
    every_length = jnp.broadcast_to(lengths[:, None], (seq_local, kv_heads)).reshape(
        seq_local * kv_heads
    )
    pair_length = lax.dynamic_slice_in_dim(every_length, pair_begin, pair_count, 0)
    scores = (
        jnp.einsum(
            "pgd,ptd->pgt",
            query_vectors,
            key_value_cache[..., :head_size],
            preferred_element_type=jnp.float32,
        )
        * score_scale
    )
    own_score = (
        jnp.einsum(
            "pgd,pd->pg", query_vectors, own_rows[:, :head_size], preferred_element_type=jnp.float32
        )
        * score_scale
    )
    visible = (
        lax.broadcasted_iota(jnp.int32, (1, 1, key_value_cache.shape[1]), 2)
        < pair_length[:, None, None]
    )
    peak = jnp.maximum(jnp.max(jnp.where(visible, scores, -1e30), -1), own_score)
    attention_weights = jnp.where(visible, jnp.exp(scores - peak[..., None]), 0.0)
    own_weight = jnp.exp(own_score - peak)
    denominator = jnp.sum(attention_weights, -1) + own_weight
    weighted = jnp.einsum(
        "pgt,ptd->pgd",
        attention_weights.astype(jnp.bfloat16),
        key_value_cache[..., head_size:],
        preferred_element_type=jnp.float32,
    )
    own_rounded = lax.optimization_barrier(own_weight.astype(jnp.bfloat16)).astype(jnp.float32)
    weighted = weighted + own_rounded[..., None] * own_rows[:, None, head_size:].astype(jnp.float32)
    head_result = (weighted / denominator[..., None]).reshape(
        pair_count, query_group_width * head_size
    )
    gathered = lax.all_gather(head_result, "tensor", axis=0, tiled=True)
    attention = gathered.reshape(seq_local, q_heads * head_size)
    updated = (residual.astype(jnp.float32) + attention).astype(jnp.bfloat16)
    stream = updated.astype(jnp.float32)
    normed = (
        stream * lax.rsqrt(jnp.mean(stream * stream, -1, keepdims=True) + 1e-05) * norm_gain
    ).astype(jnp.bfloat16)
    logits = jnp.dot(normed, router_weight, preferred_element_type=jnp.float32)
    expert_count = router_weight.shape[1]
    expert_ids = lax.broadcasted_iota(jnp.int32, (1, 1, expert_count), 2)
    chosen_mask = routing[:, :, None] == expert_ids
    chosen_logits = jnp.sum(jnp.where(chosen_mask, logits[:, None, :], 0.0), -1)
    gate_weights = jax.nn.sigmoid(chosen_logits - chosen_logits[:, ::-1])
    columns = lax.all_to_all(normed, "group", split_axis=1, concat_axis=0, tiled=True)
    gate_part = jnp.einsum("td,edf->tef", columns, expert_gate, preferred_element_type=jnp.float32)
    up_part = jnp.einsum("td,edf->tef", columns, expert_up, preferred_element_type=jnp.float32)
    summed = lax.psum_scatter(
        jnp.stack((gate_part, up_part), 2).astype(jnp.bfloat16),
        "group",
        scatter_dimension=0,
        tiled=True,
    ).astype(jnp.float32)
    picked = jnp.sum(jnp.where(chosen_mask[:, :, :, None, None], summed[:, None], 0.0), 2)
    expert_hidden = (
        gate_weights[:, :, None] * jax.nn.silu(picked[:, :, 0]) * picked[:, :, 1]
    ).astype(jnp.bfloat16)
    return (updated, expert_hidden, new_cache)


def solution(mesh):
    in_specs = (
        P(("group", "tensor"), None, None),
        P("group", None, None),
        P("group", None, None),
        P("group"),
        P("group", None),
        P(),
        P(),
        P("group", None),
        P(None, "group", "tensor"),
        P(None, "group", "tensor"),
    )
    out_specs = (P("group", None), P("group", None, "tensor"), P("group", None, "tensor", None))
    return jax.shard_map(body, mesh=mesh, in_specs=in_specs, out_specs=out_specs, check_vma=False)
```

profile of v0, /device:TPU:0, one launch (start us, length us, event | category | flops | bytes accessed | tf_op | source)
XLA Modules:
  0.0 109.6 jit_solution(10600744194444090793)
XLA Ops:
  7.2 0.8 broadcast_in_dim.87
  8.0 0.1 reshape.106
  8.1 0.1 iota_compare_fusion
  8.2 0.9 reshape.107
  9.2 0.7 dynamic-slice_convert_fusion
  9.9 0.1 fusion.30
  10.0 2.3 %select_reduce_fusion.1 = (f32[8,6]{1,0:T(8,128)S(1)}, f32[8,6,1024]{2,1,0:T(8,128)S(1)}) fusion(pred[8,1024]{1,0:T(8,128)(4,1)S(1)} %iota_compare_fusion, bf16[8,1024,256]{2,1,0:T(8,128)(2,1)} %param.10, bf16[64,6,128]{2,1,0:T(8,128)(2,1)S(1)} %reshape.107, s32[]{:T(128)S(6)} %select_n.24), kind=kOutput, calls=%fused_computation.18 | convolution fusion | flops 12730320 | bytes 2318532 | tf_op jit(solution)/shard_map/pgd,ptd->pgt/dot_general | solution.py:49
  12.3 0.2 fusion.18
  12.6 2.0 %fusion.15 = f32[1,8,6,128]{3,2,1,0:T(8,128)S(1)} fusion(bf16[8,1024,256]{2,1,0:T(8,128)(2,1)} %param.10, f32[8,6,1024]{2,1,0:T(8,128)S(1)} %get-tuple-element.21, f32[8,6]{1,0:T(8,128)S(1)} %multiply_maximum_fusion, pred[8,1024]{1,0:T(8,128)(4,1)S(1)} %iota_compare_fusion, f32[8,6]{1,0:T(8,128)S(1)} %get-tuple-element.19, ...), kind=kOutput, calls=%fused_computation.12 | convolution fusion | flops 12748800 | bytes 2331200 | tf_op jit(solution)/shard_map/pgt,ptd->pgd/dot_general | solution.py:71
  14.6 10.7 %all_gather.3 = f32[64,768]{1,0:T(8,128)S(1)} all-gather(f32[8,768]{1,0:T(8,128)S(1)} %bitcast.58), channel_id=1, replica_groups=mesh['group'=4,'tensor'=8] {'tensor'}, dimensions={0}, use_global_device_ids=true | all-gather | bytes 221184 | tf_op jit(solution)/shard_map/all_gather | solution.py:82
  25.4 0.2 fusion.20
  25.6 0.7 fusion.22
  26.4 4.9 %all-to-all-start = ((bf16[8,4,1536]{2,0,1:T(8,128)(2,1)}), bf16[8,4,1536]{2,0,1:T(8,128)(2,1)S(1)}, u32[]{:S(2)}, u32[]{:S(2)}) async-start(bf16[8,4,1536]{2,0,1:T(8,128)(2,1)} %bitcast.4), calls=%async_computation | async-start | bytes 196608 | tf_op jit(solution)/shard_map/all_to_all | solution.py:95
  31.2 6.6 %copy.30 = bf16[8,1024,256]{2,0,1:T(8,128)(2,1)} copy(bf16[8,1024,256]{2,1,0:T(8,128)(2,1)} %param.10) | data formatting | bytes 8388608 | tf_op args[0]
  37.8 4.5 %all-to-all-start.1 = ((bf16[8,1024,256]{2,0,1:T(8,128)(2,1)}), bf16[8,1024,256]{2,0,1:T(8,128)(2,1)}, u32[]{:S(2)}, u32[]{:S(2)}) async-start(bf16[8,1024,256]{2,0,1:T(8,128)(2,1)} %copy.30), calls=%async_computation.1 | async-start | bytes 8388608 | tf_op jit(solution)/shard_map/all_to_all | solution.py:27
  42.4 10.6 %fusion.4 = bf16[32,8,1,1024]{3,0,1,2:T(8,128)(2,1)S(1)} fusion(bf16[8,1536,1024]{2,1,0:T(8,128)(2,1)} %param.18, bf16[8,4,1536]{2,0,1:T(8,128)(2,1)S(1)} %all-to-all-done), kind=kOutput, calls=%fused_computation.7 | convolution fusion | flops 805568512 | bytes 25788416 | tf_op jit(solution)/shard_map/td,edf->tef/dot_general | solution.py:96
  53.0 10.6 %fusion.5 = bf16[32,8,1,1024]{3,0,1,2:T(8,128)(2,1)S(1)} fusion(bf16[8,1536,1024]{2,1,0:T(8,128)(2,1)} %param.19, bf16[8,4,1536]{2,0,1:T(8,128)(2,1)S(1)} %all-to-all-done), kind=kOutput, calls=%fused_computation.8 | convolution fusion | flops 805568512 | bytes 25788416 | tf_op jit(solution)/shard_map/td,edf->tef/dot_general | solution.py:97
  63.6 0.1 pad_maximum_fusion
  63.7 1.1 copy.40
  64.9 1.1 fusion.40
  66.0 0.2 select_reduce_fusion.2
  66.2 0.1 copy.25
  66.3 27.7 %reduce-scatter.4.cloned.1.call-done = bf16[8,16384]{1,0:T(8,128)(2,1)} async-done(((bf16[32,16384]{1,0:T(8,128)(2,1)}), bf16[8,16384]{1,0:T(8,128)(2,1)}) %reduce-scatter.4.cloned.1.call-update) | async-done | bytes 262160
  94.0 1.1 %copy.52 = bf16[1,8,16,1024]{3,2,1,0:T(8,128)(2,1)S(1)} copy(bf16[1,8,16,1024]{3,1,2,0:T(8,128)(2,1)} %bitcast.57) | data formatting | bytes 524288
  95.1 0.2 copy_convert_fusion
  95.3 0.3 copy.27
  95.6 0.4 select_reduce_fusion
  96.0 0.1 fusion.39
  96.1 0.7 fusion.29
  96.8 3.1 %copy.31 = bf16[8,1024,256]{2,1,0:T(8,128)(2,1)S(1)} copy(bf16[8,1024,256]{2,0,1:T(8,128)(2,1)} %all-to-all-done.1) | data formatting | bytes 8388608 | tf_op jit(solution)/shard_map/all_to_all | solution.py:27
  99.9 0.4 broadcast_select_fusion
  100.3 2.5 %copy.32 = bf16[8,8,128,256]{3,2,1,0:T(8,128)(2,1)} copy(bf16[8,8,128,256]{3,2,0,1:T(8,128)(2,1)S(1)} %broadcast_select_fusion) | data formatting | bytes 8388608
  (32 shorter events, 0.5 us)
Async XLA Ops:
  7.2 57.7 %copy-start = (bf16[6144,8]{0,1:T(8,128)(2,1)S(1)}, bf16[6144,8]{0,1:T(8,128)(2,1)}, u32[]{:S(2)}) copy-start(bf16[6144,8]{0,1:T(8,128)(2,1)} %param.16) | copy-start | bytes 294916
  7.2 18.2 %copy-start.2 = (bf16[8,6144]{1,0:T(8,128)(2,1)S(1)}, bf16[8,6144]{1,0:T(8,128)(2,1)}, u32[]{:S(2)}) copy-start(bf16[8,6144]{1,0:T(8,128)(2,1)} %param.14) | copy-start | bytes 294916
  7.2 18.4 %copy-start.4 = (f32[6144]{0:T(1024)S(1)}, f32[6144]{0:T(1024)}, u32[]{:S(2)}) copy-start(f32[6144]{0:T(1024)} %param.15) | copy-start | bytes 73732
  25.6 12.2 %copy-start.1 = (bf16[8,6144]{1,0:T(8,128)(2,1)}, bf16[8,6144]{1,0:T(8,128)(2,1)S(1)}, u32[]{:S(2)}) copy-start(bf16[8,6144]{1,0:T(8,128)(2,1)S(1)} %get-tuple-element.13) | copy-start | bytes 294916
  26.4 11.4 %all-to-all-start = ((bf16[8,4,1536]{2,0,1:T(8,128)(2,1)}), bf16[8,4,1536]{2,0,1:T(8,128)(2,1)S(1)}, u32[]{:S(2)}, u32[]{:S(2)}) async-start(bf16[8,4,1536]{2,0,1:T(8,128)(2,1)} %bitcast.4), calls=%async_computation | async-start | bytes 196608 | tf_op jit(solution)/shard_map/all_to_all | solution.py:95
  37.8 59.0 %all-to-all-start.1 = ((bf16[8,1024,256]{2,0,1:T(8,128)(2,1)}), bf16[8,1024,256]{2,0,1:T(8,128)(2,1)}, u32[]{:S(2)}, u32[]{:S(2)}) async-start(bf16[8,1024,256]{2,0,1:T(8,128)(2,1)} %copy.30), calls=%async_computation.1 | async-start | bytes 8388608 | tf_op jit(solution)/shard_map/all_to_all | solution.py:27
  42.3 51.7 %reduce-scatter.4.cloned.1.call-start = ((), (), s32[]{:S(2)}) async-start(), calls=%async_computation.3 | async-start | bytes 1310720
  63.6 1.2 %copy-start.3 = (bf16[8,8,256]{2,1,0:T(8,128)(2,1)S(1)}, bf16[8,8,256]{2,1,0:T(8,128)(2,1)}, u32[]{:S(2)}) copy-start(bf16[8,8,256]{2,1,0:T(8,128)(2,1)} %param.12) | copy-start | bytes 98308
  63.6 1.2 %copy-start.5 = (s32[8,2]{0,1:T(2,128)S(1)}, s32[8,2]{0,1:T(2,128)}, u32[]{:S(2)}) copy-start(s32[8,2]{0,1:T(2,128)} %param.17) | copy-start | bytes 196
  63.6 2.7 %copy-start.6 = (s32[8]{0:T(128)S(1)}, s32[8]{0:T(128)}, u32[]{:S(2)}) copy-start(s32[8]{0:T(128)} %param.13) | copy-start | bytes 100
Sparse Core Ops, SparseCore 0:
  64.9 29.0 reduce-scatter.3
where the time goes:
time: 110 us
  waiting for transfers between devices  27.7 us (25%)
  matrix products  26.7 us (24%)
  local copies, waits for them, and re-layouts  16.8 us (15%)
  between operations  14.2 us (13%)
  blocking collectives  10.7 us (10%)
  starting transfers between devices  9.45 us (9%)
  other arithmetic  4.03 us (4%)
    unnamed x2, waiting for transfers between devices  27.7 us
    unnamed x20, local copies, waits for them, and re-layouts  11.3 us
    all_gather x1, blocking collectives, body(): gathered = lax.all_gather(head_result, 'tensor', axis=0, tiled=True)  10.7 us
    dot_general x1, matrix products, body(): jnp.einsum('td,edf->tef', columns, expert_gate, preferred_element_type=jn...  10.6 us
    dot_general x1, matrix products, body(): jnp.einsum('td,edf->tef', columns, expert_up, preferred_element_type=jnp....  10.6 us
    all_to_all x1, starting transfers between devices, body(): lax.all_to_all(normed, 'group', split_axis=1, concat_axis=0, tiled=True)  4.87 us
    all_to_all x1, starting transfers between devices, body(): lax.all_to_all(key_value_cache, 'tensor', split_axis=1, concat_axis=0, ti...  4.54 us
    all_to_all x1, local copies, waits for them, and re-layouts, body(): lax.all_to_all(key_value_cache, 'tensor', split_axis=1, concat_axis=0, ti...  3.05 us
  transfers between devices with their start and end apart: 3, of which 1 were waited for; matrix products, arithmetic and copies ran while one was open for 30% of the time, Pallas kernels for 0%

commit v1 on v0

--- a/solution.py
+++ b/solution.py
@@ -79,7 +79,10 @@
     head_result = (weighted / denominator[..., None]).reshape(
         pair_count, query_group_width * head_size
     )
-    gathered = lax.all_gather(head_result, "tensor", axis=0, tiled=True)
+    gathered = jnp.concatenate(
+        lax.all_to_all(jnp.stack([head_result] * lax.axis_size("tensor"), axis=0), "tensor", 0, 0),
+        axis=0,
+    )
     attention = gathered.reshape(seq_local, q_heads * head_size)
     updated = (residual.astype(jnp.float32) + attention).astype(jnp.bfloat16)
     stream = updated.astype(jnp.float32)

time: 110 us -> 111 us (level)
    all_to_all x0 -> x1, blocking collectives: none -> 11.2 us  [body(): lax.all_to_all(jnp.stack([head_result] * lax.axis_size('tensor'), axis=0)...]
    all_gather x1 -> x0, blocking collectives: 10.7 us -> none  [body(): gathered = lax.all_gather(head_result, 'tensor', axis=0, tiled=True)]
    unnamed x20 -> x21, local copies, waits for them, and re-layouts: 11.3 us -> 11.4 us
where the time goes in v1:
time: 111 us; the launch traced here: 110 us
  waiting for transfers between devices  27.7 us (25%)
  matrix products  26.7 us (24%)
  local copies, waits for them, and re-layouts  16.8 us (15%)
  between operations  14.3 us (13%)
  blocking collectives  11.2 us (10%)
  starting transfers between devices  9.45 us (9%)
  other arithmetic  4.04 us (4%)
    unnamed x2, waiting for transfers between devices  27.7 us
    unnamed x21, local copies, waits for them, and re-layouts  11.4 us
    all_to_all x1, blocking collectives, body(): lax.all_to_all(jnp.stack([head_result] * lax.axis_size('tensor'), axis=0)...  11.2 us
    dot_general x1, matrix products, body(): jnp.einsum('td,edf->tef', columns, expert_gate, preferred_element_type=jn...  10.6 us
    dot_general x1, matrix products, body(): jnp.einsum('td,edf->tef', columns, expert_up, preferred_element_type=jnp....  10.6 us
    all_to_all x1, starting transfers between devices, body(): lax.all_to_all(normed, 'group', split_axis=1, concat_axis=0, tiled=True)  4.87 us
    all_to_all x1, starting transfers between devices, body(): lax.all_to_all(key_value_cache, 'tensor', split_axis=1, concat_axis=0, ti...  4.54 us
    all_to_all x1, local copies, waits for them, and re-layouts, body(): lax.all_to_all(key_value_cache, 'tensor', split_axis=1, concat_axis=0, ti...  3.05 us
  transfers between devices with their start and end apart: 3, of which 1 were waited for; matrix products, arithmetic and copies ran while one was open for 30% of the time, Pallas kernels for 0%

profile of v1, /device:TPU:0, one launch (start us, length us, event | category | flops | bytes accessed | tf_op | source)
XLA Modules:
  0.0 110.2 jit_solution(12860447726771310441)
XLA Ops:
  7.2 0.8 broadcast_in_dim.87
  8.0 0.1 reshape.102
  8.1 0.1 iota_compare_fusion
  8.2 0.9 reshape.103
  9.2 0.7 dynamic-slice_convert_fusion
  9.9 0.1 fusion.30
  10.0 2.3 %select_reduce_fusion.1 = (f32[8,6]{1,0:T(8,128)S(1)}, f32[8,6,1024]{2,1,0:T(8,128)S(1)}) fusion(pred[8,1024]{1,0:T(8,128)(4,1)S(1)} %iota_compare_fusion, bf16[8,1024,256]{2,1,0:T(8,128)(2,1)} %param.10, bf16[64,6,128]{2,1,0:T(8,128)(2,1)S(1)} %reshape.103, s32[]{:T(128)S(6)} %select_n.24), kind=kOutput, calls=%fused_computation.18 | convolution fusion | flops 12730320 | bytes 2318532 | tf_op jit(solution)/shard_map/pgd,ptd->pgt/dot_general | solution.py:49
  12.3 0.2 fusion.18
  12.6 2.0 %fusion.15 = f32[1,8,6,128]{3,2,1,0:T(8,128)S(1)} fusion(bf16[8,1024,256]{2,1,0:T(8,128)(2,1)} %param.10, f32[8,6,1024]{2,1,0:T(8,128)S(1)} %get-tuple-element.21, f32[8,6]{1,0:T(8,128)S(1)} %multiply_maximum_fusion, pred[8,1024]{1,0:T(8,128)(4,1)S(1)} %iota_compare_fusion, f32[8,6]{1,0:T(8,128)S(1)} %get-tuple-element.19, ...), kind=kOutput, calls=%fused_computation.12 | convolution fusion | flops 12748800 | bytes 2331200 | tf_op jit(solution)/shard_map/pgt,ptd->pgd/dot_general | solution.py:71
  14.6 11.2 %all_to_all.39 = f32[8,8,768]{2,1,0:T(8,128)S(1)} all-to-all(f32[8,8,768]{2,1,0:T(8,128)S(1)} %stack.15), channel_id=1, replica_groups=mesh['group'=4,'tensor'=8] {'tensor'}, dimensions={0} | all-to-all | bytes 393216 | tf_op jit(solution)/shard_map/all_to_all | solution.py:83
  25.9 0.2 fusion.20
  26.1 0.7 fusion.22
  26.9 4.9 %all-to-all-start.1 = ((bf16[8,4,1536]{2,0,1:T(8,128)(2,1)}), bf16[8,4,1536]{2,0,1:T(8,128)(2,1)S(1)}, u32[]{:S(2)}, u32[]{:S(2)}) async-start(bf16[8,4,1536]{2,0,1:T(8,128)(2,1)} %bitcast.4), calls=%async_computation.1 | async-start | bytes 196608 | tf_op jit(solution)/shard_map/all_to_all | solution.py:98
  31.7 6.6 %copy.30 = bf16[8,1024,256]{2,0,1:T(8,128)(2,1)} copy(bf16[8,1024,256]{2,1,0:T(8,128)(2,1)} %param.10) | data formatting | bytes 8388608 | tf_op args[0]
  38.3 4.5 %all-to-all-start.2 = ((bf16[8,1024,256]{2,0,1:T(8,128)(2,1)}), bf16[8,1024,256]{2,0,1:T(8,128)(2,1)}, u32[]{:S(2)}, u32[]{:S(2)}) async-start(bf16[8,1024,256]{2,0,1:T(8,128)(2,1)} %copy.30), calls=%async_computation.2 | async-start | bytes 8388608 | tf_op jit(solution)/shard_map/all_to_all | solution.py:27
  42.9 10.6 %fusion.4 = bf16[32,8,1,1024]{3,0,1,2:T(8,128)(2,1)S(1)} fusion(bf16[8,1536,1024]{2,1,0:T(8,128)(2,1)} %param.18, bf16[8,4,1536]{2,0,1:T(8,128)(2,1)S(1)} %all-to-all-done.1), kind=kOutput, calls=%fused_computation.7 | convolution fusion | flops 805568512 | bytes 25788416 | tf_op jit(solution)/shard_map/td,edf->tef/dot_general | solution.py:99
  53.5 10.6 %fusion.5 = bf16[32,8,1,1024]{3,0,1,2:T(8,128)(2,1)S(1)} fusion(bf16[8,1536,1024]{2,1,0:T(8,128)(2,1)} %param.19, bf16[8,4,1536]{2,0,1:T(8,128)(2,1)S(1)} %all-to-all-done.1), kind=kOutput, calls=%fused_computation.8 | convolution fusion | flops 805568512 | bytes 25788416 | tf_op jit(solution)/shard_map/td,edf->tef/dot_general | solution.py:100
  64.1 0.1 pad_maximum_fusion
  64.2 1.1 copy.41
  65.5 1.1 fusion.40
  66.6 0.2 select_reduce_fusion.2
  66.8 0.1 copy.25
  66.8 27.7 %reduce-scatter.4.cloned.1.call-done = bf16[8,16384]{1,0:T(8,128)(2,1)} async-done(((bf16[32,16384]{1,0:T(8,128)(2,1)}), bf16[8,16384]{1,0:T(8,128)(2,1)}) %reduce-scatter.4.cloned.1.call-update) | async-done | bytes 262160
  94.5 1.1 copy.53
  95.6 0.2 copy_convert_fusion
  95.8 0.3 copy.27
  96.1 0.4 select_reduce_fusion
  96.5 0.1 fusion.39
  96.6 0.7 fusion.29
  97.4 3.1 %copy.31 = bf16[8,1024,256]{2,1,0:T(8,128)(2,1)S(1)} copy(bf16[8,1024,256]{2,0,1:T(8,128)(2,1)} %all-to-all-done.2) | data formatting | bytes 8388608 | tf_op jit(solution)/shard_map/all_to_all | solution.py:27
  100.4 0.4 broadcast_select_fusion
  100.8 2.5 %copy.32 = bf16[8,8,128,256]{3,2,1,0:T(8,128)(2,1)} copy(bf16[8,8,128,256]{3,2,0,1:T(8,128)(2,1)S(1)} %broadcast_select_fusion) | data formatting | bytes 8388608
  (33 shorter events, 0.5 us)
Async XLA Ops:
  7.2 58.3 %copy-start = (bf16[6144,8]{0,1:T(8,128)(2,1)S(1)}, bf16[6144,8]{0,1:T(8,128)(2,1)}, u32[]{:S(2)}) copy-start(bf16[6144,8]{0,1:T(8,128)(2,1)} %param.16) | copy-start | bytes 294916
  7.2 18.7 %copy-start.2 = (bf16[8,6144]{1,0:T(8,128)(2,1)S(1)}, bf16[8,6144]{1,0:T(8,128)(2,1)}, u32[]{:S(2)}) copy-start(bf16[8,6144]{1,0:T(8,128)(2,1)} %param.14) | copy-start | bytes 294916
  7.2 18.9 %copy-start.4 = (f32[6144]{0:T(1024)S(1)}, f32[6144]{0:T(1024)}, u32[]{:S(2)}) copy-start(f32[6144]{0:T(1024)} %param.15) | copy-start | bytes 73732
  26.1 12.2 %copy-start.1 = (bf16[8,6144]{1,0:T(8,128)(2,1)}, bf16[8,6144]{1,0:T(8,128)(2,1)S(1)}, u32[]{:S(2)}) copy-start(bf16[8,6144]{1,0:T(8,128)(2,1)S(1)} %get-tuple-element.13) | copy-start | bytes 294916
  26.9 11.4 %all-to-all-start.1 = ((bf16[8,4,1536]{2,0,1:T(8,128)(2,1)}), bf16[8,4,1536]{2,0,1:T(8,128)(2,1)S(1)}, u32[]{:S(2)}, u32[]{:S(2)}) async-start(bf16[8,4,1536]{2,0,1:T(8,128)(2,1)} %bitcast.4), calls=%async_computation.1 | async-start | bytes 196608 | tf_op jit(solution)/shard_map/all_to_all | solution.py:98
  38.3 59.0 %all-to-all-start.2 = ((bf16[8,1024,256]{2,0,1:T(8,128)(2,1)}), bf16[8,1024,256]{2,0,1:T(8,128)(2,1)}, u32[]{:S(2)}, u32[]{:S(2)}) async-start(bf16[8,1024,256]{2,0,1:T(8,128)(2,1)} %copy.30), calls=%async_computation.2 | async-start | bytes 8388608 | tf_op jit(solution)/shard_map/all_to_all | solution.py:27
  42.9 51.7 %reduce-scatter.4.cloned.1.call-start = ((), (), s32[]{:S(2)}) async-start(), calls=%async_computation.4 | async-start | bytes 1310720
  64.1 1.2 %copy-start.3 = (bf16[8,8,256]{2,1,0:T(8,128)(2,1)S(1)}, bf16[8,8,256]{2,1,0:T(8,128)(2,1)}, u32[]{:S(2)}) copy-start(bf16[8,8,256]{2,1,0:T(8,128)(2,1)} %param.12) | copy-start | bytes 98308
  64.1 1.2 %copy-start.5 = (s32[8,2]{0,1:T(2,128)S(1)}, s32[8,2]{0,1:T(2,128)}, u32[]{:S(2)}) copy-start(s32[8,2]{0,1:T(2,128)} %param.17) | copy-start | bytes 196
  64.1 1.3 %copy-start.6 = (s32[8]{0:T(128)S(1)}, s32[8]{0:T(128)}, u32[]{:S(2)}) copy-start(s32[8]{0:T(128)} %param.13) | copy-start | bytes 100
Sparse Core Ops, SparseCore 0:
  65.4 29.0 reduce-scatter.3
